TPU v7x, 32 devices: a whole 2x2x4 slice. The times are simulated.
32 devices in a mesh: rep: 4 (over x, y), dp: 8 (over z, core).
Axes of the slice: x: 2, y: 2, z: 4, core: 2. Of those that a mesh axis runs over, the one named last changes fastest.
Arguments:
- x: bfloat16 [32, 1024, 512], P(('rep', 'dp')), parts along dimension 0
- dy: bfloat16 [32, 1024, 512], P(('rep', 'dp')), parts along dimension 0
- w_gate: bfloat16 [2, 512, 8192], P(None, 'dp')
- w_up: bfloat16 [2, 512, 8192], P(None, 'dp')
- w_down: bfloat16 [2, 8192, 512], P(None, 'dp')
- m_w_gate: float32 [2, 512, 8192], P(None, 'dp')
- m_w_up: float32 [2, 512, 8192], P(None, 'dp')
- m_w_down: float32 [2, 8192, 512], P(None, 'dp')
- v_w_gate: float32 [2, 512, 8192], P(None, 'dp')
- v_w_up: float32 [2, 512, 8192], P(None, 'dp')
- v_w_down: float32 [2, 8192, 512], P(None, 'dp')
Outputs:
- output 1: bfloat16 [8, 512, 8192], P('rep', 'dp'), parts along dimension 0
- output 2: bfloat16 [8, 512, 8192], P('rep', 'dp'), parts along dimension 0
- output 3: bfloat16 [8, 8192, 512], P('rep', 'dp'), parts along dimension 0
- output 4: float32 [8, 512, 8192], P('rep', 'dp'), parts along dimension 0
- output 5: float32 [8, 512, 8192], P('rep', 'dp'), parts along dimension 0
- output 6: float32 [8, 8192, 512], P('rep', 'dp'), parts along dimension 0
- output 7: float32 [8, 512, 8192], P('rep', 'dp'), parts along dimension 0
- output 8: float32 [8, 512, 8192], P('rep', 'dp'), parts along dimension 0
- output 9: float32 [8, 8192, 512], P('rep', 'dp'), parts along dimension 0
There are 4 independent parts. A program takes and returns all parts, laid end to end along the dimension named above; an argument that names none is the same for every part.
All inputs are finite; a program needn't handle non-finite values.
Results may differ from a plain program's by a relative error of at most 0.022.
Values are sent between devices in bfloat16 or wider.
A program may use at most 2 GiB of HBM per device.

v0:
```python
import jax
import jax.numpy as jnp
from jax import lax
from jax.sharding import PartitionSpec as P

NAMES = ("w_gate", "w_up", "w_down")


def matmul(a, w):
    return jnp.dot(a, w, preferred_element_type=jnp.float32).astype(jnp.bfloat16)


def normed(h):
    wide = h.astype(jnp.float32)
    scale = lax.rsqrt(jnp.mean(wide**2, -1, keepdims=True) + 1e-6)
    return (wide * scale).astype(jnp.bfloat16)


def layer(h, w):
    a = normed(h)
    gate = jnp.dot(a, w["w_gate"], preferred_element_type=jnp.float32)
    up = jnp.dot(a, w["w_up"], preferred_element_type=jnp.float32)
    return h + matmul((jax.nn.silu(gate) * up).astype(jnp.bfloat16), w["w_down"])


def adamw(w, m, v, g):
    m = 0.9 * m + 0.1 * g
    v = 0.95 * v + 0.05 * g * g
    step = m * lax.rsqrt(v + 1e-8) + 0.1 * w
    return (w - 0.02 * step).astype(jnp.bfloat16), m, v


def clipped(gradients, sum_of_squares, count):
    factor = jnp.minimum(1.0, 0.5 * lax.rsqrt(sum_of_squares / count + 1e-30))
    return [g * factor for g in gradients]


def solution(mesh):
    def fetched(weights, number):
        return {name: lax.all_gather(w[number], "dp", axis=0, tiled=True) for name, w in zip(NAMES, weights, strict=True)}

    def step(x, dy, *arrays):
        weights, m, v = (arrays[i : i + 3] for i in (0, 3, 6))
        layers = weights[0].shape[0]
        h, kept = x[0], []
        for number in range(layers):
            kept.append(h)
            h = layer(h, fetched(weights, number))
        by_h, mine = dy[0], [None] * layers
        for number in reversed(range(layers)):
            _, back = jax.vjp(lambda w, h: layer(h, w), fetched(weights, number), kept[number])
            by_w, by_h = back(by_h)
            mine[number] = [lax.psum_scatter(by_w[name], "dp", scatter_dimension=0, tiled=True) for name in NAMES]
        gradients = [jnp.stack([mine[number][i] for number in range(layers)]).astype(jnp.float32) for i in range(3)]
        squares = lax.psum(sum(jnp.sum(g * g) for g in gradients), "dp")
        gradients = clipped(gradients, squares, lax.psum(1, "dp") * sum(g.size for g in gradients))
        new = [adamw(w.astype(jnp.float32), m, v, g) for w, m, v, g in zip(weights, m, v, gradients, strict=True)]
        return tuple(one[which] for which in range(3) for one in new)

    states, cut = P(("rep", "dp"), None, None), P(None, "dp", None)
    return jax.shard_map(
        step,
        mesh=mesh,
        in_specs=(states, states) + (cut,) * 9,
        out_specs=(P("rep", "dp", None),) * 9,
        check_vma=False,
    )
```

profile of v0, /device:TPU:0, one launch (start us, length us, event | category | flops | bytes accessed | tf_op | source)
XLA Modules:
  0.0 1190.4 jit_solution(6274605432952563446)
XLA Ops:
  20.2 74.7 %all-gather.13.cloned.1.call-done = bf16[1,512,8192]{2,1,0:T(8,128)(2,1)} async-done(((bf16[1,64,8192]{2,1,0:T(8,128)(2,1)}), bf16[1,512,8192]{2,1,0:T(8,128)(2,1)}) %all-gather.13.cloned.1.call-update) | async-done | bytes 8388624 | tf_op jit(solution)/shard_map/all_gather | solution.py:40
  94.8 18.7 %fusion.34 = f32[1024,8192]{1,0:T(8,128)} fusion(bf16[1,512,8192]{2,1,0:T(8,128)(2,1)} %all-gather.13.cloned.1.call-done, bf16[1,1024,512]{1,2,0:T(8,128)(2,1)S(1)} %copy.20, f32[1024]{0:T(1024)S(1)} %add_rsqrt_fusion), kind=kOutput, calls=%fused_computation.45 | convolution fusion | flops 8591507456 | bytes 42995712 | tf_op jit(solution)/shard_map/dot_general | solution.py:21
  113.5 63.8 %all-gather.15.cloned.1.call-done = bf16[1,512,8192]{2,1,0:T(8,128)(2,1)} async-done(((bf16[1,64,8192]{2,1,0:T(8,128)(2,1)}), bf16[1,512,8192]{2,1,0:T(8,128)(2,1)}) %all-gather.15.cloned.1.call-update) | async-done | bytes 8388624 | tf_op jit(solution)/shard_map/all_gather | solution.py:40
  177.4 33.2 %multiply_convert_fusion.1 = (bf16[1024,8192]{1,0:T(8,128)(2,1)}, f32[1024,8192]{1,0:T(8,128)}) fusion(f32[1024,8192]{1,0:T(8,128)} %fusion.34, bf16[1,512,8192]{2,1,0:T(8,128)(2,1)} %all-gather.15.cloned.1.call-done, bf16[1,1024,512]{1,2,0:T(8,128)(2,1)S(1)} %copy.20, f32[1024]{0:T(1024)S(1)} %add_rsqrt_fusion), kind=kOutput, calls=%fused_computation.17 | convolution fusion | flops 8641839104 | bytes 93327360 | tf_op jit(solution)/shard_map/dot_general | solution.py:22
  210.6 49.3 %all-gather.17.cloned.1.call-done = bf16[1,8192,512]{2,1,0:T(8,128)(2,1)} async-done(((bf16[1,1024,512]{2,1,0:T(8,128)(2,1)}), bf16[1,8192,512]{2,1,0:T(8,128)(2,1)}) %all-gather.17.cloned.1.call-update) | async-done | bytes 8388624 | tf_op jit(solution)/shard_map/all_gather | solution.py:40
  259.9 15.2 %fusion.62 = (f32[1024]{0:T(1024)S(1)}, bf16[1024,512]{0,1:T(8,128)(2,1)S(1)}) fusion(bf16[1024,8192]{1,0:T(8,128)(2,1)} %get-tuple-element.24, bf16[1,8192,512]{2,1,0:T(8,128)(2,1)} %all-gather.17.cloned.1.call-done, bf16[1,1024,512]{1,2,0:T(8,128)(2,1)S(1)} %copy.20), kind=kOutput, calls=%fused_computation.94 | convolution fusion | flops 8592555008 | bytes 27267072 | tf_op jit(solution)/shard_map/dot_general | solution.py:10
  275.2 67.1 %all-gather.21.cloned.1.call-done = bf16[1,8192,512]{2,1,0:T(8,128)(2,1)} async-done(((bf16[1,1024,512]{2,1,0:T(8,128)(2,1)}), bf16[1,8192,512]{2,1,0:T(8,128)(2,1)}) %all-gather.21.cloned.1.call-update) | async-done | bytes 8388624 | tf_op jit(solution)/shard_map/all_gather | solution.py:40
  342.3 15.2 %convolution_convert_fusion.1 = bf16[1024,8192]{1,0:T(8,128)(2,1)} fusion(bf16[1,8192,512]{2,1,0:T(8,128)(2,1)} %all-gather.21.cloned.1.call-done, bf16[1,1024,512]{2,1,0:T(8,128)(2,1)S(1)} %copy-done.13), kind=kOutput, calls=%fused_computation.25 | convolution fusion | flops 8598323200 | bytes 26214400 | tf_op jit(solution)/shard_map/transpose(jvp())/dot_general | solution.py:10
  357.5 67.2 %all-gather.23.cloned.1.call-done = bf16[1,512,8192]{2,1,0:T(8,128)(2,1)} async-done(((bf16[1,64,8192]{2,1,0:T(8,128)(2,1)}), bf16[1,512,8192]{2,1,0:T(8,128)(2,1)}) %all-gather.23.cloned.1.call-update) | async-done | bytes 8388624 | tf_op jit(solution)/shard_map/all_gather | solution.py:40
  424.7 18.7 %fusion.21 = f32[1024,8192]{1,0:T(8,128)} fusion(bf16[1,512,8192]{2,1,0:T(8,128)(2,1)} %all-gather.23.cloned.1.call-done, bf16[1024,512]{0,1:T(8,128)(2,1)S(1)} %get-tuple-element.27, f32[1024]{0:T(1024)S(1)} %fusion.91), kind=kOutput, calls=%fused_computation.32 | convolution fusion | flops 8591507456 | bytes 42995712 | tf_op jit(solution)/shard_map/jvp()/dot_general | solution.py:22
  443.4 63.7 %all-gather.19.cloned.1.call-done = bf16[1,512,8192]{2,1,0:T(8,128)(2,1)} async-done(((bf16[1,64,8192]{2,1,0:T(8,128)(2,1)}), bf16[1,512,8192]{2,1,0:T(8,128)(2,1)}) %all-gather.19.cloned.1.call-update) | async-done | bytes 8388624 | tf_op jit(solution)/shard_map/all_gather | solution.py:40
  507.1 41.0 %fusion.2 = (bf16[1024,8192]{1,0:T(8,128)(2,1)}, f32[1024,8192]{1,0:T(8,128)}) fusion(f32[1024,8192]{1,0:T(8,128)} %fusion.21, bf16[1024,8192]{1,0:T(8,128)(2,1)} %convolution_convert_fusion.1, bf16[1,512,8192]{2,1,0:T(8,128)(2,1)} %all-gather.19.cloned.1.call-done, bf16[1024,512]{0,1:T(8,128)(2,1)S(1)} %get-tuple-element.27, f32[1024]{0:T(1024)S(1)} %fusion.91), kind=kOutput, calls=%fused_computation.8 | convolution fusion | flops 8692170752 | bytes 110104576 | tf_op jit(solution)/shard_map/jvp()/dot_general | solution.py:21
  548.1 21.1 %fusion.71 = bf16[1024,512]{0,1:T(8,128)(2,1)S(1)} fusion(bf16[1,512,8192]{2,1,0:T(8,128)(2,1)} %all-gather.23.cloned.1.call-done, bf16[1024,8192]{1,0:T(8,128)(2,1)} %convolution_convert_fusion.1, f32[1024,8192]{1,0:T(8,128)} %get-tuple-element.29), kind=kOutput, calls=%fused_computation.102 | convolution fusion | flops 8640790528 | bytes 59768832 | tf_op jit(solution)/shard_map/transpose(jvp())/dot_general | solution.py:22
  569.3 12.8 %fusion.64 = (f32[1024]{0:T(1024)S(1)}, bf16[1024,512]{0,1:T(8,128)(2,1)S(1)}) fusion(bf16[1024,512]{0,1:T(8,128)(2,1)S(1)} %get-tuple-element.27, bf16[1024,512]{0,1:T(8,128)(2,1)S(1)} %fusion.71, bf16[1024,8192]{1,0:T(8,128)(2,1)} %get-tuple-element.28, bf16[1,512,8192]{2,1,0:T(8,128)(2,1)S(1)} %copy-done.21), kind=kOutput, calls=%fused_computation.96 | convolution fusion | flops 8592555008 | bytes 28315648 | tf_op jit(solution)/shard_map/transpose(jvp())/dot_general | solution.py:21
  582.9 17.4 %convolution_convert_fusion.2 = bf16[8192,512]{1,0:T(8,128)(2,1)} fusion(bf16[1024,8192]{1,0:T(8,128)(2,1)} %get-tuple-element.24, bf16[1024,512]{0,1:T(8,128)(2,1)S(1)} %fusion.80), kind=kOutput, calls=%fused_computation.30 | convolution fusion | flops 8594128896 | bytes 26214400 | tf_op jit(solution)/shard_map/transpose(jvp())/dot_general | solution.py:10
  601.5 26.8 %fusion.18 = bf16[8192,512]{1,0:T(8,128)(2,1)} fusion(f32[1024,8192]{1,0:T(8,128)} %fusion.21, bf16[1,1024,512]{2,1,0:T(8,128)(2,1)S(1)} %copy-done.14, f32[1024,8192]{1,0:T(8,128)} %get-tuple-element.29), kind=kOutput, calls=%fused_computation.27 | convolution fusion | flops 8644460544 | bytes 76546048 | tf_op jit(solution)/shard_map/transpose(jvp())/dot_general | solution.py:10
  628.4 16.1 %convolution_convert_fusion = bf16[1024,8192]{1,0:T(8,128)(2,1)} fusion(bf16[1024,512]{0,1:T(8,128)(2,1)S(1)} %fusion.80, bf16[1,8192,512]{2,1,0:T(8,128)(2,1)} %all-gather.17.cloned.1.call-done), kind=kOutput, calls=%fused_computation.24 | convolution fusion | flops 8598323200 | bytes 26214400 | tf_op jit(solution)/shard_map/transpose(jvp())/dot_general | solution.py:10
  644.5 22.3 %fusion.20 = bf16[512,8192]{1,0:T(8,128)(2,1)} fusion(bf16[1024,8192]{1,0:T(8,128)(2,1)} %convolution_convert_fusion, f32[1024,8192]{1,0:T(8,128)} %fusion.34, bf16[1,1024,512]{1,2,0:T(8,128)(2,1)S(1)} %copy-done.1, f32[1024]{0:T(1024)S(1)} %copy-done.18), kind=kOutput, calls=%fused_computation.29 | convolution fusion | flops 8646033408 | bytes 59772928 | tf_op jit(solution)/shard_map/transpose(jvp())/dot_general | solution.py:22
  668.0 22.4 %fusion.19 = bf16[512,8192]{1,0:T(8,128)(2,1)} fusion(bf16[1024,8192]{1,0:T(8,128)(2,1)} %convolution_convert_fusion.1, bf16[1024,512]{0,1:T(8,128)(2,1)S(1)} %copy-done.10, f32[1024]{0:T(1024)S(1)} %copy-done.16, f32[1024,8192]{1,0:T(8,128)} %get-tuple-element.29), kind=kOutput, calls=%fused_computation.28 | convolution fusion | flops 8646033408 | bytes 59772928 | tf_op jit(solution)/shard_map/transpose(jvp())/dot_general | solution.py:22
  690.5 32.9 %fusion.15 = bf16[512,8192]{1,0:T(8,128)(2,1)} fusion(f32[1024,8192]{1,0:T(8,128)} %fusion.34, f32[1024,8192]{1,0:T(8,128)} %get-tuple-element.25, bf16[1024,8192]{1,0:T(8,128)(2,1)} %convolution_convert_fusion, bf16[1,1024,512]{1,2,0:T(8,128)(2,1)S(1)} %copy-done.1, f32[1024]{0:T(1024)S(1)} %copy-done.18), kind=kOutput, calls=%fused_computation.26 | convolution fusion | flops 8687976448 | bytes 93327360 | tf_op jit(solution)/shard_map/transpose(jvp())/dot_general | solution.py:21
  723.5 17.1 %convolution_convert_fusion.3 = bf16[512,8192]{1,0:T(8,128)(2,1)} fusion(bf16[1024,8192]{1,0:T(8,128)(2,1)} %get-tuple-element.28, bf16[1024,512]{0,1:T(8,128)(2,1)S(1)} %copy-done.10, f32[1024]{0:T(1024)S(1)} %copy-done.16), kind=kOutput, calls=%fused_computation.31 | convolution fusion | flops 8591507456 | bytes 26218496 | tf_op jit(solution)/shard_map/transpose(jvp())/dot_general | solution.py:21
  740.7 38.5 %reduce-scatter.17.cloned.1.call-done = bf16[1024,512]{1,0:T(8,128)(2,1)} async-done(((bf16[8192,512]{1,0:T(8,128)(2,1)}), bf16[1024,512]{1,0:T(8,128)(2,1)}) %reduce-scatter.17.cloned.1.call-update) | async-done | bytes 1048592 | tf_op jit(solution)/shard_map/reduce_scatter | solution.py:53
  779.1 3.2 fusion.48
  782.4 87.2 %reduce-scatter.11.cloned.1.call-done = bf16[64,8192]{1,0:T(8,128)(2,1)} async-done(((bf16[512,8192]{1,0:T(8,128)(2,1)}), bf16[64,8192]{1,0:T(8,128)(2,1)}) %reduce-scatter.11.cloned.1.call-update) | async-done | bytes 1048592 | tf_op jit(solution)/shard_map/reduce_scatter | solution.py:53
  869.6 90.3 %reduce-scatter.13.cloned.1.call-done = bf16[64,8192]{1,0:T(8,128)(2,1)} async-done(((bf16[512,8192]{1,0:T(8,128)(2,1)}), bf16[64,8192]{1,0:T(8,128)(2,1)}) %reduce-scatter.13.cloned.1.call-update) | async-done | bytes 1048592 | tf_op jit(solution)/shard_map/reduce_scatter | solution.py:53
  959.8 3.2 fusion.47
  963.1 87.2 %reduce-scatter.7.cloned.1.call-done = bf16[64,8192]{1,0:T(8,128)(2,1)} async-done(((bf16[512,8192]{1,0:T(8,128)(2,1)}), bf16[64,8192]{1,0:T(8,128)(2,1)}) %reduce-scatter.7.cloned.1.call-update) | async-done | bytes 1048592 | tf_op jit(solution)/shard_map/reduce_scatter | solution.py:53
  1050.3 90.3 %reduce-scatter.9.cloned.1.call-done = bf16[64,8192]{1,0:T(8,128)(2,1)} async-done(((bf16[512,8192]{1,0:T(8,128)(2,1)}), bf16[64,8192]{1,0:T(8,128)(2,1)}) %reduce-scatter.9.cloned.1.call-update) | async-done | bytes 1048592 | tf_op jit(solution)/shard_map/reduce_scatter | solution.py:53
  1140.6 3.2 fusion.46
  1145.7 14.3 %psum.7 = f32[]{:T(128)} all-reduce(f32[]{:T(128)S(6)} %add.99), channel_id=1, replica_groups=mesh['rep'=4,'dp'=8] {'dp'}, use_global_device_ids=true, to_apply=%region_12.13 | all-reduce | flops 1 | bytes 8 | tf_op jit(solution)/shard_map/psum | solution.py:55
  1160.8 8.7 fusion.54
  1169.9 13.2 %fusion.45 = (bf16[2,64,8192]{2,1,0:T(8,128)(2,1)}, f32[2,64,8192]{2,1,0:T(8,128)}, f32[2,64,8192]{2,1,0:T(8,128)}, bf16[2,64,8192]{2,1,0:T(8,128)(2,1)}, f32[2,64,8192]{2,1,0:T(8,128)}, /*index=5*/f32[2,64,8192]{2,1,0:T(8,128)}) fusion(bf16[2,64,8192]{2,1,0:T(8,128)(2,1)S(1)} %copy-done.4, f32[]{:T(128)S(6)} %min_shard_map.3, ...), kind=kLoop, calls=%fused_computation.70 | loop fusion | flops 41943040 | bytes 46137348 | tf_op jit(solution)/shard_map/convert_element_type | solution.py:30
  (79 shorter events, 16.6 us)
Async XLA Ops:
  7.2 6.5 copy-start.2
  7.2 87.6 %all-gather.13.cloned.1.call-start = ((), (), s32[]{:S(2)}) async-start(), calls=%async_computation.12 | async-start | bytes 9437184 | tf_op jit(solution)/shard_map/all_gather | solution.py:40
  10.4 6.5 copy-start.12
  10.4 166.9 %all-gather.15.cloned.1.call-start = ((), (), s32[]{:S(2)}) async-start(), calls=%async_computation.13 | async-start | bytes 9437184 | tf_op jit(solution)/shard_map/all_gather | solution.py:40
  13.6 246.3 %all-gather.17.cloned.1.call-start = ((), (), s32[]{:S(2)}) async-start(), calls=%async_computation.14 | async-start | bytes 9437184 | tf_op jit(solution)/shard_map/all_gather | solution.py:40
  15.2 327.1 %all-gather.21.cloned.1.call-start = ((), (), s32[]{:S(2)}) async-start(), calls=%async_computation.16 | async-start | bytes 9437184 | tf_op jit(solution)/shard_map/all_gather | solution.py:40
  15.7 408.9 %all-gather.23.cloned.1.call-start = ((), (), s32[]{:S(2)}) async-start(), calls=%async_computation.17 | async-start | bytes 9437184 | tf_op jit(solution)/shard_map/all_gather | solution.py:40
  16.3 490.8 %all-gather.19.cloned.1.call-start = ((), (), s32[]{:S(2)}) async-start(), calls=%async_computation.15 | async-start | bytes 9437184 | tf_op jit(solution)/shard_map/all_gather | solution.py:40
  16.9 723.7 %reduce-scatter.15.cloned.1.call-start = ((), (), s32[]{:S(2)}) async-start(), calls=%async_computation.10 | async-start | bytes 9437184 | tf_op jit(solution)/shard_map/reduce_scatter | solution.py:53
  17.5 242.4 %copy-start = (bf16[1,1024,512]{1,2,0:T(8,128)(2,1)}, bf16[1,1024,512]{1,2,0:T(8,128)(2,1)S(1)}, u32[]{:S(2)}) copy-start(bf16[1,1024,512]{1,2,0:T(8,128)(2,1)S(1)} %copy.20) | copy-start | bytes 3145732
  17.8 159.6 %copy-start.17 = (f32[1024]{0:T(1024)}, f32[1024]{0:T(1024)S(1)}, u32[]{:S(2)}) copy-start(f32[1024]{0:T(1024)S(1)} %add_rsqrt_fusion) | copy-start | bytes 12292
  259.9 82.4 %copy-start.13 = (bf16[1,1024,512]{2,1,0:T(8,128)(2,1)S(1)}, bf16[1,1024,512]{2,1,0:T(8,128)(2,1)}, u32[]{:S(2)}) copy-start(bf16[1,1024,512]{2,1,0:T(8,128)(2,1)} %param.12) | copy-start | bytes 3145732
  275.2 82.3 %copy-start.19 = (f32[1024]{0:T(1024)}, f32[1024]{0:T(1024)S(1)}, u32[]{:S(2)}) copy-start(f32[1024]{0:T(1024)S(1)} %get-tuple-element.26) | copy-start | bytes 12292
  275.2 307.0 %copy-start.9 = (bf16[1024,512]{0,1:T(8,128)(2,1)}, bf16[1024,512]{0,1:T(8,128)(2,1)S(1)}, u32[]{:S(2)}) copy-start(bf16[1024,512]{0,1:T(8,128)(2,1)S(1)} %get-tuple-element.27) | copy-start | bytes 3145732
  275.2 307.0 %copy-start.15 = (f32[1024]{0:T(1024)}, f32[1024]{0:T(1024)S(1)}, u32[]{:S(2)}) copy-start(f32[1024]{0:T(1024)S(1)} %fusion.91) | copy-start | bytes 12292
  548.1 21.1 %copy-start.21 = (bf16[1,512,8192]{2,1,0:T(8,128)(2,1)S(1)}, bf16[1,512,8192]{2,1,0:T(8,128)(2,1)}, u32[]{:S(2)}) copy-start(bf16[1,512,8192]{2,1,0:T(8,128)(2,1)} %all-gather.19.cloned.1.call-done) | copy-start | bytes 25165828
  569.3 12.9 %copy-start.20 = (f32[1024]{0:T(1024)S(1)}, f32[1024]{0:T(1024)}, u32[]{:S(2)}) copy-start(f32[1024]{0:T(1024)} %copy-done.19) | copy-start | bytes 12292
  569.3 12.9 %copy-start.11 = (bf16[1,1024,512]{1,2,0:T(8,128)(2,1)S(1)}, bf16[1,1024,512]{1,2,0:T(8,128)(2,1)}, u32[]{:S(2)}) copy-start(bf16[1,1024,512]{1,2,0:T(8,128)(2,1)} %copy.21) | copy-start | bytes 3145732
  600.3 178.8 %reduce-scatter.17.cloned.1.call-start = ((), (), s32[]{:S(2)}) async-start(), calls=%async_computation.11 | async-start | bytes 9437184 | tf_op jit(solution)/shard_map/reduce_scatter | solution.py:53
  628.3 16.2 %copy-start.1 = (bf16[1,1024,512]{1,2,0:T(8,128)(2,1)S(1)}, bf16[1,1024,512]{1,2,0:T(8,128)(2,1)}, u32[]{:S(2)}) copy-start(bf16[1,1024,512]{1,2,0:T(8,128)(2,1)} %copy-done) | copy-start | bytes 3145732
  628.3 16.1 %copy-start.18 = (f32[1024]{0:T(1024)S(1)}, f32[1024]{0:T(1024)}, u32[]{:S(2)}) copy-start(f32[1024]{0:T(1024)} %copy-done.17) | copy-start | bytes 12292
  628.3 241.2 %reduce-scatter.11.cloned.1.call-start = ((), (), s32[]{:S(2)}) async-start(), calls=%async_computation.8 | async-start | bytes 9437184 | tf_op jit(solution)/shard_map/reduce_scatter | solution.py:53
  666.8 1.2 copy-start.16
  666.8 293.1 %reduce-scatter.13.cloned.1.call-start = ((), (), s32[]{:S(2)}) async-start(), calls=%async_computation.9 | async-start | bytes 9437184 | tf_op jit(solution)/shard_map/reduce_scatter | solution.py:53
  690.5 359.8 %reduce-scatter.7.cloned.1.call-start = ((), (), s32[]{:S(2)}) async-start(), calls=%async_computation.6 | async-start | bytes 9437184 | tf_op jit(solution)/shard_map/reduce_scatter | solution.py:53
  723.4 417.1 %reduce-scatter.9.cloned.1.call-start = ((), (), s32[]{:S(2)}) async-start(), calls=%async_computation.7 | async-start | bytes 9437184 | tf_op jit(solution)/shard_map/reduce_scatter | solution.py:53
  740.6 420.1 %copy-start.3 = (bf16[2,1024,512]{2,1,0:T(8,128)(2,1)S(1)}, bf16[2,1024,512]{2,1,0:T(8,128)(2,1)}, u32[]{:S(2)}) copy-start(bf16[2,1024,512]{2,1,0:T(8,128)(2,1)} %param.15) | copy-start | bytes 6291460
  1160.8 8.8 copy-start.4
  1160.8 8.8 copy-start.5
  1160.8 8.8 copy-start.6
  1160.8 8.8 copy-start.7
  1160.8 9.1 copy-start.8
  (2 other events, 2.5 us)
Sparse Core Ops, SparseCore 0:
  10.6 84.1 all-gather.12
  97.0 80.3 all-gather.14
  179.5 80.3 all-gather.16
  261.9 80.3 all-gather.20
  344.3 80.3 all-gather.22
  426.7 80.3 all-gather.18
  600.5 88.2 reduce-scatter.14
  691.0 88.0 reduce-scatter.16
  781.5 88.0 reduce-scatter.10
  871.7 88.0 reduce-scatter.12
  962.1 88.0 reduce-scatter.6
  1052.4 88.0 reduce-scatter.8
where the time goes:
time: 1200 us; the launch traced here: 1190 us
  waiting for transfers between devices  781 us (65%)
  matrix products  331 us (28%)
  other arithmetic  32.6 us (3%)
  between operations  17.6 us (1%)
  blocking collectives  14.3 us (1%)
  local copies, waits for them, and re-layouts  13.4 us (1%)
    reduce_scatter x6, waiting for transfers between devices, step(): lax.psum_scatter(by_w[name], 'dp', scatter_dimension=0, tiled=True)  393 us
    all_gather x6, waiting for transfers between devices, fetched(): lax.all_gather(w[number], 'dp', axis=0, tiled=True)  386 us
    dot_general x5, matrix products, layer(): gate = jnp.dot(a, w['w_gate'], preferred_element_type=jnp.float32)  123 us
    dot_general x5, matrix products, layer(): up = jnp.dot(a, w['w_up'], preferred_element_type=jnp.float32)  118 us
    dot_general x5, matrix products, matmul(): jnp.dot(a, w, preferred_element_type=jnp.float32).astype(jnp.bfloat16)  90.6 us
  transfers between devices with their start and end apart: 12, of which 11 were waited for; matrix products, arithmetic and copies ran while one was open for 21% of the time, Pallas kernels for 0%

commit v1 on v0

v1 whole, which is shorter than its diff:
```python
import jax
import jax.numpy as jnp
from jax import lax
from jax.experimental import pallas as pl
from jax.experimental.pallas import tpu as pltpu
from jax.sharding import Mesh, PartitionSpec as P

ANY = pl.ANY
REPS, ZS, CORES = 4, 4, 2


PARTS = ((0, 0), (1, 0), (2, 0), (2, 1))


def gather_kernel(*refs):
    n = len(PARTS)
    weights, outs, held = refs[:3], refs[3 : 3 + n], refs[3 + n : 3 + 2 * n]
    ld, st, ps, pr, sa, ra, sb, rb, sc, rc = refs[3 + 2 * n :]
    ins = [weights[which].at[layer] for which, layer in PARTS]
    r, z, c = (lax.axis_index(axis) for axis in ("rep", "z", "core"))
    d = z * 2 + c
    partner = d + 1 - 2 * c
    barrier = pltpu.get_barrier_semaphore()

    def at(rep, dp):
        return (rep, dp // 2, dp % 2)

    def up(k):
        return lax.rem(z + k, ZS) * 2 + c

    def col(k):
        return lax.rem(r + k, REPS)

    near = [at(r, partner)] + [at(r, up(k)) for k in (1, 2, 3)] + [at(col(k), d) for k in (1, 2, 3)]
    loads = [pltpu.make_async_copy(i, h, ld.at[m]) for m, (i, h) in enumerate(zip(ins, held))]
    for one in loads:
        one.start()
    for one in near:
        pl.semaphore_signal(barrier, inc=1, device_id=one, device_id_type=pl.DeviceIdType.MESH)
    pl.semaphore_wait(barrier, len(near))

    def quarter(ref, m, owner, q):
        rows = ref.shape[0] // (8 if owner is not None else 1)
        first = 0 if owner is None else owner * rows
        if PARTS[m][0] < 2:
            wide = ref.shape[1] // REPS
            return ref.at[pl.ds(first, rows), pl.ds(pl.multiple_of(q * wide, wide), wide)]
        deep = rows // REPS
        return ref.at[pl.ds(pl.multiple_of(first + q * deep, deep), deep), :]

    def shard(ref, owner):
        rows = ref.shape[0] // 8
        return ref.at[pl.ds(pl.multiple_of(owner * rows, rows), rows), :]

    def remote(src, dst, s, t, to):
        return pltpu.make_async_remote_copy(src_ref=src, dst_ref=dst, send_sem=s, recv_sem=t, device_id=to, device_id_type=pl.DeviceIdType.MESH)

    started = []
    own = []
    for m in range(n):
        loads[m].wait()
        for k in (1, 3, 2):
            one = remote(quarter(held[m], m, None, r), quarter(outs[m], m, d, r), sa.at[m, k - 1], ra.at[m, k - 1], at(r, up(k)))
            one.start()
            started.append(one)
        one = remote(held[m], shard(outs[m], d), ps.at[m], pr.at[m], at(r, partner))
        one.start()
        started.append(one)
        mine = pltpu.make_async_copy(held[m], shard(outs[m], d), st.at[m])
        mine.start()
        own.append(mine)
    for m in range(n):
        for k in (1, 3, 2):
            src = lax.rem(z + ZS - k, ZS) * 2 + c
            piece = quarter(outs[m], m, src, r)
            remote(quarter(held[m], m, None, r), piece, sa.at[m, k - 1], ra.at[m, k - 1], at(r, up(k))).wait_recv()
            for j in (3, 1, 2):
                one = remote(piece, piece, sb.at[m, k - 1, j - 1], rb.at[m, k - 1, j - 1], at(col(j), d))
                one.start()
                started.append(one)
    for m in range(n):
        for k in (1, 3, 2):
            src = lax.rem(z + ZS - k, ZS) * 2 + c
            for j in (3, 1, 2):
                piece = quarter(outs[m], m, src, lax.rem(r + REPS - j, REPS))
                remote(piece, piece, sb.at[m, k - 1, j - 1], rb.at[m, k - 1, j - 1], at(col(j), d)).wait_recv()
            one = remote(shard(outs[m], src), shard(outs[m], src), sc.at[m, k - 1], rc.at[m, k - 1], at(r, partner))
            one.start()
            started.append(one)
    for m in range(n):
        remote(held[m], shard(outs[m], partner), ps.at[m], pr.at[m], at(r, partner)).wait_recv()
        for k in (1, 3, 2):
            src = lax.rem(z + ZS - k, ZS) * 2 + 1 - c
            remote(shard(outs[m], src), shard(outs[m], src), sc.at[m, k - 1], rc.at[m, k - 1], at(r, partner)).wait_recv()
    for one in own:
        one.wait()
    for one in started:
        one.wait_send()


def gather(weights, collective_id):
    dma = pltpu.SemaphoreType.DMA
    n, shards = len(PARTS), [weights[which].shape[1:] for which, _ in PARTS]
    return pl.pallas_call(
        gather_kernel,
        out_shape=[jax.ShapeDtypeStruct((ZS * CORES * rows, columns), jnp.bfloat16) for rows, columns in shards],
        in_specs=[pl.BlockSpec(memory_space=ANY)] * 3,
        out_specs=[pl.BlockSpec(memory_space=ANY)] * n,
        scratch_shapes=[pltpu.VMEM(shape, jnp.bfloat16) for shape in shards]
        + [dma((n,))] * 4
        + [dma((n, 3))] * 2
        + [dma((n, 3, 3))] * 2
        + [dma((n, 3))] * 2,
        compiler_params=pltpu.CompilerParams(collective_id=collective_id, has_side_effects=True),
        name="gather",
    )(*weights)


def matmul(a, w):
    return jnp.dot(a, w, preferred_element_type=jnp.float32).astype(jnp.bfloat16)


def over_tokens(a, b):
    return lax.dot_general(a, b, (((0,), (0,)), ((), ())), preferred_element_type=jnp.float32).astype(jnp.bfloat16)


def back_to(a, w):
    return lax.dot_general(a, w, (((1,), (1,)), ((), ())), preferred_element_type=jnp.float32).astype(jnp.bfloat16)


def normed(h):
    wide = h.astype(jnp.float32)
    scale = lax.rsqrt(jnp.mean(wide**2, -1, keepdims=True) + 1e-6)
    return (wide * scale).astype(jnp.bfloat16)


def gated(gate, up):
    return (jax.nn.silu(gate) * up).astype(jnp.bfloat16)


def projection_kernel(a, w_gate, w_up, gate, up, hidden):
    gate[...] = jnp.dot(a[...], w_gate[...], preferred_element_type=jnp.float32)
    up[...] = jnp.dot(a[...], w_up[...], preferred_element_type=jnp.float32)
    hidden[...] = gated(gate[...], up[...])


def projections(a, w):
    (tokens, d), ff, tile = a.shape, w[0].shape[1], 512
    wide = pl.BlockSpec((tokens, tile), lambda i: (0, i))
    return pl.pallas_call(
        projection_kernel,
        grid=(ff // tile,),
        out_shape=[jax.ShapeDtypeStruct((tokens, ff), kind) for kind in (jnp.float32, jnp.float32, jnp.bfloat16)],
        in_specs=[pl.BlockSpec((tokens, d), lambda i: (0, 0))] + [pl.BlockSpec((d, tile), lambda i: (0, i))] * 2,
        out_specs=[wide] * 3,
        cost_estimate=pl.CostEstimate(flops=4 * tokens * d * ff, bytes_accessed=10 * tokens * ff + 4 * d * ff, transcendentals=tokens * ff),
        name="projections",
    )(a, w[0], w[1])


def input_kernel(by_gate, by_up, w_gate, w_up, token, by_a, of_gate, of_up):
    @pl.when(pl.program_id(0) == 0)
    def _():
        of_gate[...] = jnp.zeros_like(of_gate)
        of_up[...] = jnp.zeros_like(of_up)

    across = (((1,), (1,)), ((), ()))
    of_gate[...] += lax.dot_general(by_gate[...], w_gate[...], across, preferred_element_type=jnp.float32)
    of_up[...] += lax.dot_general(by_up[...], w_up[...], across, preferred_element_type=jnp.float32)

    @pl.when(pl.program_id(0) == pl.num_programs(0) - 1)
    def _():
        wide = of_gate[...].astype(jnp.bfloat16).astype(jnp.float32) + of_up[...].astype(jnp.bfloat16).astype(jnp.float32)
        by_a[...] = wide.astype(jnp.bfloat16)


def back_to_input(by_gate, by_up, w, token):
    (tokens, ff), d, tile = by_gate.shape, w[0].shape[0], 512
    return pl.pallas_call(
        input_kernel,
        grid=(ff // tile,),
        out_shape=jax.ShapeDtypeStruct((tokens, d), jnp.bfloat16),
        in_specs=[pl.BlockSpec((tokens, tile), lambda i: (0, i))] * 2
        + [pl.BlockSpec((d, tile), lambda i: (0, i))] * 2
        + [pl.BlockSpec(memory_space=ANY)],
        out_specs=pl.BlockSpec((tokens, d), lambda i: (0, 0)),
        scratch_shapes=[pltpu.VMEM((tokens, d), jnp.float32)] * 2,
        cost_estimate=pl.CostEstimate(flops=4 * tokens * d * ff, bytes_accessed=4 * ff * (tokens + d), transcendentals=0),
        name="back_to_input",
    )(by_gate, by_up, w[0], w[1], token)


def total_kernel(x, out, slots, send, recv):
    r, z, c = (lax.axis_index(axis) for axis in ("rep", "z", "core"))
    n, d = ZS * CORES, z * CORES + c
    barrier = pltpu.get_barrier_semaphore()

    def to(k):
        other = lax.rem(d + k, n)
        return (r, other // CORES, other % CORES)

    for k in range(1, n):
        pl.semaphore_signal(barrier, inc=1, device_id=to(k), device_id_type=pl.DeviceIdType.MESH)
    pl.semaphore_wait(barrier, n - 1)
    copies = [
        pltpu.make_async_remote_copy(
            src_ref=x, dst_ref=slots.at[d], send_sem=send.at[k - 1], recv_sem=recv.at[k - 1], device_id=to(k), device_id_type=pl.DeviceIdType.MESH
        )
        for k in range(1, n)
    ]
    for one in copies:
        one.start()
    slots[d] = x[...]
    for one in copies:
        one.wait()
    out[...] = sum(slots[i] for i in range(n))


def total(x, collective_id):
    shape = (8, 128)
    return pl.pallas_call(
        total_kernel,
        out_shape=jax.ShapeDtypeStruct(shape, jnp.float32),
        in_specs=[pl.BlockSpec(memory_space=pltpu.VMEM)],
        out_specs=pl.BlockSpec(memory_space=pltpu.VMEM),
        scratch_shapes=[pltpu.VMEM((ZS * CORES,) + shape, jnp.float32)] + [pltpu.SemaphoreType.DMA((ZS * CORES - 1,))] * 2,
        compiler_params=pltpu.CompilerParams(collective_id=collective_id, has_side_effects=True),
        name="total",
    )(jnp.broadcast_to(x, shape))[0, 0]


def after_kernel(x, token, y):
    y[...] = x[...]


def after(x, token):
    return pl.pallas_call(
        after_kernel,
        out_shape=jax.ShapeDtypeStruct(x.shape, x.dtype),
        in_specs=[pl.BlockSpec(memory_space=pltpu.VMEM), pl.BlockSpec(memory_space=ANY)],
        out_specs=pl.BlockSpec(memory_space=pltpu.VMEM),
        name="after",
    )(x, token)


def adamw(w, m, v, g):
    m = 0.9 * m + 0.1 * g
    v = 0.95 * v + 0.05 * g * g
    step = m * lax.rsqrt(v + 1e-8) + 0.1 * w
    return (w - 0.02 * step).astype(jnp.bfloat16), m, v


def solution(mesh):
    cells = Mesh(mesh.devices.reshape(REPS, ZS, CORES), ("rep", "z", "core"))
    everyone, line = ("rep", "z", "core"), ("z", "core")

    def backward(h, by_h, w, kept, deeper):
        a, from_a = jax.vjp(normed, h)
        gate, up, hidden = kept(a, w)
        down = over_tokens(hidden, by_h)
        scattered = [lax.psum_scatter(down, line, scatter_dimension=0, tiled=True)]
        by_h = after(by_h, down)
        by_gate, by_up = (by.astype(jnp.bfloat16) for by in jax.vjp(gated, gate, up)[1](back_to(by_h, w[2])))
        both = jnp.concatenate([over_tokens(a, by_gate), over_tokens(a, by_up)], axis=1)
        summed = lax.psum_scatter(both, line, scatter_dimension=0, tiled=True)
        by_x = from_a(back_to_input(by_gate, by_up, w, both))[0] + by_h if deeper else None
        return jnp.split(summed, 2, axis=1) + scattered, by_x

    def step(x, dy, *arrays):
        weights, m, v = (arrays[i : i + 3] for i in (0, 3, 6))
        *first, last_down = gather(weights, 3)
        second = [lax.all_gather(w[1], line, axis=0, tiled=True) for w in weights[:2]] + [last_down]
        x, dy = x[0], dy[0]
        lowest = projections(normed(x), first)
        h = x + matmul(lowest[2], first[2])
        late, by_h = backward(h, dy, second, projections, True)
        early, _ = backward(x, by_h, first, lambda a, w: lowest, False)
        early[2] = after(early[2], late[0])
        squares = total(sum(jnp.sum(g.astype(jnp.float32) ** 2) for g in late + early), 4)
        mine = [jnp.stack([e, l]).astype(jnp.float32) for e, l in zip(early, late)]
        count = sum(g.size for g in mine) * ZS * CORES
        factor = jnp.minimum(1.0, 0.5 * lax.rsqrt(squares / count + 1e-30))
        new = [adamw(w.astype(jnp.float32), m, v, g * factor) for w, m, v, g in zip(weights, m, v, mine, strict=True)]
        return tuple(one[which] for which in range(3) for one in new)

    states, cut = P(everyone, None, None), P(None, line, None)
    return jax.shard_map(
        step,
        mesh=cells,
        in_specs=(states, states) + (cut,) * 9,
        out_specs=(P("rep", line, None),) * 9,
        check_vma=False,
    )
```

time: 1200 us -> 884 us (0.74)
  waiting for transfers between devices: 781 us -> 276 us
  Pallas kernels: 0 us -> 308 us
  matrix products: 331 us -> 191 us
  other arithmetic: 32.6 us -> 64.7 us
  blocking collectives: 14.3 us -> 0 us
    all_gather x6 -> x2, waiting for transfers between devices: 386 us -> 0.01 us  [step(): lax.all_gather(w[1], line, axis=0, tiled=True)]
    pallas_call x0 -> x8, Pallas kernels: none -> 308 us  [the longest x1 199 us: gather(): pl.pallas_call(gather_kernel, out_shape=[jax.ShapeDtypeStruct((ZS * CORES...]
    reduce_scatter x6 -> x4, waiting for transfers between devices: 393 us -> 276 us  [the longest x2 193 us: backward(): summed = lax.psum_scatter(both, line, scatter_dimension=0, tiled=True)]
    dot_general x5 -> x1, matrix products: 90.6 us -> 14.9 us  [matmul(): jnp.dot(a, w, preferred_element_type=jnp.float32).astype(jnp.bfloat16)]
    dot_general x10 -> x8, matrix products: 240 us -> 176 us  [the longest x6 121 us: over_tokens(): lax.dot_general(a, b, (((0,), (0,)), ((), ())), preferred_element_type=jn...]
    concatenate x0 -> x2, other arithmetic: none -> 27.4 us  [backward(): jnp.concatenate([over_tokens(a, by_gate), over_tokens(a, by_up)], axis=1)]
    psum x1 -> x0, blocking collectives: 14.3 us -> none  [step(): squares = lax.psum(sum((jnp.sum(g * g) for g in gradients)), 'dp')]
  transfers between devices with their start and end apart: 12 -> 6, of which waited for: 11 -> 3; matrix products, arithmetic and copies ran while one was open for 21% -> 25% of each run, Pallas kernels for 0% -> 31%
where the time goes in v1:
time: 884 us; the launch traced here: 874 us
  Pallas kernels  308 us (35%)
  waiting for transfers between devices  276 us (31%)
  matrix products  191 us (22%)
  other arithmetic  64.7 us (7%)
  between operations  19.4 us (2%)
  local copies, waits for them, and re-layouts  13.9 us (2%)
    pallas_call x1, Pallas kernels, gather(): pl.pallas_call(gather_kernel, out_shape=[jax.ShapeDtypeStruct((ZS * CORES...  199 us
    reduce_scatter x2, waiting for transfers between devices, backward(): summed = lax.psum_scatter(both, line, scatter_dimension=0, tiled=True)  193 us
    dot_general x6, matrix products, over_tokens(): lax.dot_general(a, b, (((0,), (0,)), ((), ())), preferred_element_type=jn...  121 us
    reduce_scatter x2, waiting for transfers between devices, backward(): scattered = [lax.psum_scatter(down, line, scatter_dimension=0, tiled=True)]  82.4 us
    pallas_call x2, Pallas kernels, projections(): pl.pallas_call(projection_kernel, grid=(ff // tile,), out_shape=[jax.Shap...  66.5 us
    dot_general x2, matrix products, back_to(): lax.dot_general(a, w, (((1,), (1,)), ((), ())), preferred_element_type=jn...  55.4 us
    pallas_call x1, Pallas kernels, back_to_input(): pl.pallas_call(input_kernel, grid=(ff // tile,), out_shape=jax.ShapeDtype...  28.9 us
    concatenate x2, other arithmetic, backward(): jnp.concatenate([over_tokens(a, by_gate), over_tokens(a, by_up)], axis=1)  27.4 us
  transfers between devices with their start and end apart: 6, of which 3 were waited for; matrix products, arithmetic and copies ran while one was open for 25% of the time, Pallas kernels for 31%

profile of v1, /device:TPU:0, one launch (start us, length us, event | category | flops | bytes accessed | tf_op | source)
XLA Modules:
  0.0 873.7 jit_solution(407313563717508716)
XLA Ops:
  7.2 2.3 slice.9
  9.6 2.3 slice.10
  11.9 198.9 %gather.1 = (bf16[512,8192]{1,0:T(8,128)(2,1)}, bf16[512,8192]{1,0:T(8,128)(2,1)}, bf16[8192,512]{1,0:T(8,128)(2,1)}, bf16[8192,512]{1,0:T(8,128)(2,1)}) custom-call(bf16[2,64,8192]{2,1,0:T(8,128)(2,1)} %refs_0_.1, bf16[2,64,8192]{2,1,0:T(8,128)(2,1)} %refs_1_.1, bf16[2,1024,512]{2,1,0:T(8,128)(2,1)} %refs_2_.1), custom_call_target="tpu_custom_call" | custom-call | tf_op jit(solution)/shard_map/gather/pallas_call | solution.py:104
  212.4 33.2 %projections.2 = (f32[1024,8192]{1,0:T(8,128)}, f32[1024,8192]{1,0:T(8,128)}, bf16[1024,8192]{1,0:T(8,128)(2,1)}) custom-call(bf16[1024,512]{1,0:T(8,128)(2,1)} %fusion.31.a, bf16[512,8192]{1,0:T(8,128)(2,1)} %get-tuple-element.19.w_gate, bf16[512,8192]{1,0:T(8,128)(2,1)} %get-tuple-element.20.w_up), custom_call_target="tpu_custom_call" | custom-call | flops 17179869184 | bytes 100663296 | tf_op jit(solution)/shard_map/projections/pallas_call | solution.py:150
  245.6 14.9 %fusion.34 = (f32[1024]{0:T(1024)S(1)}, bf16[1024,512]{1,0:T(8,128)(2,1)S(1)}) fusion(bf16[1024,8192]{1,0:T(8,128)(2,1)} %get-tuple-element.21, bf16[8192,512]{1,0:T(8,128)(2,1)} %get-tuple-element.22, bf16[1,1024,512]{2,1,0:T(8,128)(2,1)S(1)} %copy-done.7), kind=kOutput, calls=%fused_computation.66 | convolution fusion | flops 8592555008 | bytes 27267072 | tf_op jit(solution)/shard_map/dot_general | solution.py:120
  263.0 33.3 %projections.3 = (f32[1024,8192]{1,0:T(8,128)}, f32[1024,8192]{1,0:T(8,128)}, bf16[1024,8192]{1,0:T(8,128)(2,1)}) custom-call(bf16[1024,512]{1,0:T(8,128)(2,1)} %fusion.35.a, bf16[512,8192]{1,0:T(8,128)(2,1)} %bitcast.36, bf16[512,8192]{1,0:T(8,128)(2,1)} %bitcast.38), custom_call_target="tpu_custom_call" | custom-call | flops 17179869184 | bytes 100663296 | tf_op jit(solution)/shard_map/projections/pallas_call | solution.py:150
  296.3 17.5 %convolution_convert_fusion.5.token = bf16[8192,512]{1,0:T(8,128)(2,1)} fusion(bf16[1024,8192]{1,0:T(8,128)(2,1)} %get-tuple-element.23, bf16[1,1024,512]{2,1,0:T(8,128)(2,1)S(1)} %copy-done.10), kind=kOutput, calls=%fused_computation.26 | convolution fusion | flops 8594128896 | bytes 26214400 | tf_op jit(solution)/shard_map/dot_general | solution.py:124
  314.3 2.3 after.3
  316.6 40.1 %fusion.4 = (bf16[1024,8192]{1,0:T(8,128)(2,1)}, bf16[1024,8192]{1,0:T(8,128)(2,1)}) fusion(f32[1024,8192]{1,0:T(8,128)} %get-tuple-element.26, f32[1024,8192]{1,0:T(8,128)} %get-tuple-element.25, bf16[1024,512]{1,0:T(8,128)(2,1)} %after.3, bf16[8192,512]{1,0:T(8,128)(2,1)} %get-tuple-element.24), kind=kOutput, calls=%fused_computation.10 | convolution fusion | flops 8724152320 | bytes 110100480 | tf_op jit(solution)/shard_map/dot_general | solution.py:128
  356.7 17.1 %convolution_convert_fusion.4 = bf16[512,8192]{1,0:T(8,128)(2,1)} fusion(bf16[1024,512]{1,0:T(8,128)(2,1)S(1)} %copy-done.13, bf16[1024,8192]{1,0:T(8,128)(2,1)} %get-tuple-element.42.by_gate), kind=kOutput, calls=%fused_computation.25 | convolution fusion | flops 8594128896 | bytes 26214400 | tf_op jit(solution)/shard_map/dot_general | solution.py:124
  373.8 11.6 %convolution_convert_fusion.3 = bf16[512,8192]{1,0:T(8,128)(2,1)} fusion(bf16[1024,512]{1,0:T(8,128)(2,1)S(1)} %copy-done.13, bf16[1024,8192]{1,0:T(8,128)(2,1)S(1)} %copy-done), kind=kOutput, calls=%fused_computation.24 | convolution fusion | flops 8594128896 | bytes 26214400 | tf_op jit(solution)/shard_map/dot_general | solution.py:124
  385.5 13.6 %pad_maximum_fusion.token = bf16[512,16384]{1,0:T(8,128)(2,1)} fusion(bf16[512,8192]{1,0:T(8,128)(2,1)} %convolution_convert_fusion.3, bf16[512,8192]{1,0:T(8,128)(2,1)} %convolution_convert_fusion.4), kind=kLoop, calls=%fused_computation.16 | loop fusion | flops 33554432 | bytes 33554432 | tf_op jit(solution)/shard_map/concatenate | solution.py:264
  399.4 28.9 %back_to_input.1 = bf16[1024,512]{1,0:T(8,128)(2,1)} custom-call(bf16[1024,8192]{1,0:T(8,128)(2,1)} %get-tuple-element.42.by_gate, bf16[1024,8192]{1,0:T(8,128)(2,1)} %get-tuple-element.43.by_up, bf16[512,8192]{1,0:T(8,128)(2,1)} %bitcast.37, bf16[512,8192]{1,0:T(8,128)(2,1)} %bitcast.39, bf16[512,16384]{1,0:T(8,128)(2,1)} %pad_maximum_fusion.token), custom_call_target="tpu_custom_call" | custom-call | flops 17179869184 | bytes 50331648 | tf_op jit(solution)/shard_map/back_to_input/pallas_call | solution.py:179
  429.8 1.8 fusion.38.x
  431.6 17.8 %convolution_convert_fusion.2.token = bf16[8192,512]{1,0:T(8,128)(2,1)} fusion(bf16[1024,8192]{1,0:T(8,128)(2,1)} %get-tuple-element.21, bf16[1024,512]{1,0:T(8,128)(2,1)S(1)} %fusion.38.x), kind=kOutput, calls=%fused_computation.23 | convolution fusion | flops 8594128896 | bytes 26214400 | tf_op jit(solution)/shard_map/dot_general | solution.py:124
  449.5 2.3 after.4
  453.0 15.2 %convolution_convert_fusion = bf16[1024,8192]{1,0:T(8,128)(2,1)} fusion(bf16[1024,512]{1,0:T(8,128)(2,1)S(1)} %copy-done.11, bf16[8192,512]{1,0:T(8,128)(2,1)} %get-tuple-element.22), kind=kOutput, calls=%fused_computation.20 | convolution fusion | flops 8598323200 | bytes 26214400 | tf_op jit(solution)/shard_map/dot_general | solution.py:128
  468.2 23.7 %fusion.15 = bf16[512,8192]{1,0:T(8,128)(2,1)} fusion(bf16[1024,512]{1,0:T(8,128)(2,1)S(1)} %copy-done.12, bf16[1024,8192]{1,0:T(8,128)(2,1)} %convolution_convert_fusion, f32[1024,8192]{1,0:T(8,128)} %get-tuple-element.28), kind=kOutput, calls=%fused_computation.27 | convolution fusion | flops 8652849152 | bytes 59768832 | tf_op jit(solution)/shard_map/dot_general | solution.py:124
  491.9 33.1 %fusion.12 = bf16[512,8192]{1,0:T(8,128)(2,1)} fusion(bf16[1024,512]{1,0:T(8,128)(2,1)S(1)} %copy-done.12, f32[1024,8192]{1,0:T(8,128)} %get-tuple-element.28, f32[1024,8192]{1,0:T(8,128)} %get-tuple-element.27, bf16[1024,8192]{1,0:T(8,128)(2,1)} %convolution_convert_fusion), kind=kOutput, calls=%fused_computation.22 | convolution fusion | flops 8694792192 | bytes 93323264 | tf_op jit(solution)/shard_map/dot_general | solution.py:124
  524.9 13.8 %pad_maximum_fusion.1 = bf16[512,16384]{1,0:T(8,128)(2,1)} fusion(bf16[512,8192]{1,0:T(8,128)(2,1)} %fusion.15, bf16[512,8192]{1,0:T(8,128)(2,1)} %fusion.12), kind=kLoop, calls=%fused_computation.17 | loop fusion | flops 33554432 | bytes 33554432 | tf_op jit(solution)/shard_map/concatenate | solution.py:264
  538.8 2.4 multiply_reduce_fusion.3
  541.1 28.7 %reduce-scatter.7.cloned.1.call-done = bf16[64,16384]{1,0:T(8,128)(2,1)} async-done(((bf16[512,16384]{1,0:T(8,128)(2,1)}), bf16[64,16384]{1,0:T(8,128)(2,1)}) %reduce-scatter.7.cloned.1.call-update) | async-done | bytes 2097168 | tf_op jit(solution)/shard_map/reduce_scatter | solution.py:265
  569.9 2.7 multiply_reduce_fusion.4
  574.5 3.3 slice_bitcast_fusion.1
  577.8 82.4 %reduce-scatter.11.cloned.1.call-done.x = bf16[1024,512]{1,0:T(8,128)(2,1)} async-done(((bf16[8192,512]{1,0:T(8,128)(2,1)}), bf16[1024,512]{1,0:T(8,128)(2,1)}) %reduce-scatter.11.cloned.1.call-update) | async-done | bytes 1048592 | tf_op jit(solution)/shard_map/reduce_scatter | solution.py:261
  660.2 2.3 after.5
  662.4 2.4 multiply_reduce_fusion
  664.8 164.3 %reduce-scatter.5.cloned.1.call-done = bf16[64,16384]{1,0:T(8,128)(2,1)} async-done(((bf16[512,16384]{1,0:T(8,128)(2,1)}), bf16[64,16384]{1,0:T(8,128)(2,1)}) %reduce-scatter.5.cloned.1.call-update) | async-done | bytes 2097168 | tf_op jit(solution)/shard_map/reduce_scatter | solution.py:265
  829.1 2.7 multiply_reduce_fusion.1
  834.4 6.8 total.1
  843.1 7.9 fusion.26
  853.2 13.2 %fusion.20 = (bf16[2,64,8192]{2,1,0:T(8,128)(2,1)}, f32[2,64,8192]{2,1,0:T(8,128)}, f32[2,64,8192]{2,1,0:T(8,128)}, bf16[2,64,8192]{2,1,0:T(8,128)(2,1)}, f32[2,64,8192]{2,1,0:T(8,128)}, /*index=5*/f32[2,64,8192]{2,1,0:T(8,128)}) fusion(bf16[2,64,8192]{2,1,0:T(8,128)(2,1)S(1)} %copy-done.1, f32[]{:T(128)} %bitcast.6, ...), kind=kLoop, calls=%fused_computation.39 | loop fusion | flops 41943040 | bytes 46137348 | tf_op jit(solution)/shard_map/convert_element_type | solution.py:250
  (61 shorter events, 11.8 us)
Async XLA Ops:
  7.2 255.8 %all-gather.5.cloned.1.call-start = ((), (), s32[]{:S(2)}) async-start(), calls=%async_computation.8 | async-start | bytes 9437184 | tf_op jit(solution)/shard_map/all_gather | solution.py:272
  9.5 253.5 %all-gather.7.cloned.1.call-start = ((), (), s32[]{:S(2)}) async-start(), calls=%async_computation.9 | async-start | bytes 9437184 | tf_op jit(solution)/shard_map/all_gather | solution.py:272
  11.8 199.0 %copy-start.7 = (bf16[1,1024,512]{2,1,0:T(8,128)(2,1)S(1)}, bf16[1,1024,512]{2,1,0:T(8,128)(2,1)}, u32[]{:S(2)}) copy-start(bf16[1,1024,512]{2,1,0:T(8,128)(2,1)} %param.11) | copy-start | bytes 3145732
  11.9 526.9 %reduce-scatter.9.cloned.1.call-start = ((), (), s32[]{:S(2)}) async-start(), calls=%async_computation.6 | async-start | bytes 9437184 | tf_op jit(solution)/shard_map/reduce_scatter | solution.py:261
  260.5 0.6 copy-start.16
  260.6 1.0 copy-start.3
  261.1 0.6 copy-start.14
  263.0 33.3 %copy-start.10 = (bf16[1,1024,512]{2,1,0:T(8,128)(2,1)S(1)}, bf16[1,1024,512]{2,1,0:T(8,128)(2,1)}, u32[]{:S(2)}) copy-start(bf16[1,1024,512]{2,1,0:T(8,128)(2,1)} %param.12) | copy-start | bytes 3145732
  313.8 256.1 %reduce-scatter.7.cloned.1.call-start = ((), (), s32[]{:S(2)}) async-start(), calls=%async_computation.5 | async-start | bytes 18874368 | tf_op jit(solution)/shard_map/reduce_scatter | solution.py:265
  316.6 40.2 %copy-start.13 = (bf16[1024,512]{1,0:T(8,128)(2,1)S(1)}, bf16[1024,512]{1,0:T(8,128)(2,1)}, u32[]{:S(2)}) copy-start(bf16[1024,512]{1,0:T(8,128)(2,1)} %fusion.35.a) | copy-start | bytes 3145732
  356.7 17.1 %copy-start = (bf16[1024,8192]{1,0:T(8,128)(2,1)S(1)}, bf16[1024,8192]{1,0:T(8,128)(2,1)}, u32[]{:S(2)}) copy-start(bf16[1024,8192]{1,0:T(8,128)(2,1)} %get-tuple-element.43.by_up) | copy-start | bytes 50331652
  399.1 29.1 %copy-start.4 = (bf16[1024,512]{1,0:T(8,128)(2,1)S(1)}, bf16[1024,512]{1,0:T(8,128)(2,1)}, u32[]{:S(2)}) copy-start(bf16[1024,512]{1,0:T(8,128)(2,1)} %copy-done.3) | copy-start | bytes 3145732
  399.1 30.7 %copy-start.17 = (f32[1024]{0:T(1024)S(1)}, f32[1024]{0:T(1024)}, u32[]{:S(2)}) copy-start(f32[1024]{0:T(1024)} %copy-done.16) | copy-start | bytes 12292
  399.1 30.7 %copy-start.8 = (bf16[1024,512]{1,0:T(8,128)(2,1)S(1)}, bf16[1024,512]{1,0:T(8,128)(2,1)}, u32[]{:S(2)}) copy-start(bf16[1024,512]{1,0:T(8,128)(2,1)} %after.3) | copy-start | bytes 3145732
  399.1 30.7 %copy-start.15 = (f32[1024]{0:T(1024)S(1)}, f32[1024]{0:T(1024)}, u32[]{:S(2)}) copy-start(f32[1024]{0:T(1024)} %copy-done.14) | copy-start | bytes 12292
  399.1 261.0 %reduce-scatter.11.cloned.1.call-start = ((), (), s32[]{:S(2)}) async-start(), calls=%async_computation.7 | async-start | bytes 9437184 | tf_op jit(solution)/shard_map/reduce_scatter | solution.py:261
  431.6 17.9 %copy-start.9 = (bf16[1024,512]{1,0:T(8,128)(2,1)}, bf16[1024,512]{1,0:T(8,128)(2,1)S(1)}, u32[]{:S(2)}) copy-start(bf16[1024,512]{1,0:T(8,128)(2,1)S(1)} %fusion.38.x) | copy-start | bytes 3145732
  451.7 1.2 copy-start.11
  451.8 16.4 %copy-start.12 = (bf16[1024,512]{1,0:T(8,128)(2,1)S(1)}, bf16[1024,512]{1,0:T(8,128)(2,1)}, u32[]{:S(2)}) copy-start(bf16[1024,512]{1,0:T(8,128)(2,1)} %fusion.31.a) | copy-start | bytes 3145732
  451.8 377.4 %reduce-scatter.5.cloned.1.call-start = ((), (), s32[]{:S(2)}) async-start(), calls=%async_computation.4 | async-start | bytes 18874368 | tf_op jit(solution)/shard_map/reduce_scatter | solution.py:265
  577.8 265.4 %copy-start.5 = (bf16[2,1024,512]{2,1,0:T(8,128)(2,1)S(1)}, bf16[2,1024,512]{2,1,0:T(8,128)(2,1)}, u32[]{:S(2)}) copy-start(bf16[2,1024,512]{2,1,0:T(8,128)(2,1)} %refs_2_.1) | copy-start | bytes 6291460
  843.1 7.9 copy-start.6
  851.0 1.6 copy-start.1
  851.0 2.2 copy-start.2
Sparse Core Ops, SparseCore 0:
  10.2 158.3 all-gather.4
  170.7 84.4 all-gather.6
  313.9 86.9 reduce-scatter.8
  403.1 166.7 reduce-scatter.6
  572.0 88.1 reduce-scatter.10
  662.4 166.7 reduce-scatter.4
